TPU v7x, 32 devices: a whole 2x2x4 slice. The times are simulated.
32 devices in a mesh: chan: 16 (over z, y, core), wall: 2 (over x).
Axes of the slice: x: 2, y: 2, z: 4, core: 2. Of those that a mesh axis runs over, the one named last changes fastest.
Arguments:
- coords: float32 [3, 16, 2, 4096], P(None, 'chan', 'wall'), as said below
- masses: float32 [16, 2, 4096], P('chan', 'wall'), may hold values from 0.5 to 2
- counts: int32 [16, 2, 16], P('chan', 'wall'), may hold values from 64 to 256
- lists: int32 [16, 2, 5, 16, 2], P('chan', 'wall'), may hold values from 0 to 47, as said below
Outputs:
- density: float32 [16, 2, 4096], P('chan', 'wall')
Inputs may be any that keep to these rules, and one draw needn't show every extreme that they name: `lists`: each row of 2 entries names different tiles; tile t of extended slab s is s * 16 + t, slab 0 the lower cross-wall neighbour, 1 the slab itself, 2 the upper neighbour. `coords`: channel components lie in [0, 1), cross-wall and depth components in [0, 8).
All inputs are finite; a program needn't handle non-finite values.
Results may differ from a plain program's by a relative error of at most 0.0003.
Values sent between devices are 32-bit elements; how exact they have to be, the bound alone decides.
A program may use at most 64 MiB of HBM per device.

v0:
```python
import functools
import math

import jax
import jax.numpy as jnp
from jax import lax
from jax.experimental import pallas as pl
from jax.experimental.pallas import tpu as pltpu
from jax.sharding import PartitionSpec as P

NB = 2
R = 4
LANES = 128
ROWS = 32
SHIFT = 5
PIECE = 32
MESH = pl.DeviceIdType.MESH


def wall_cases(wall, walls):
    return [(0, wall - 1, wall > 0), (1, wall + 1, wall < walls - 1)]


def arrange(
    wall, walls, tiles, tile_len, lists_ref, names_ref, tally_ref, sizes_ref, grid_ref, codes_ref
):
    list_len = lists_ref.shape[1]
    lines = codes_ref.shape[0]
    used = (R + 1) * list_len
    top = tile_len // ROWS
    shape = (lines, LANES)
    grid_ref[...] = jnp.zeros_like(grid_ref)
    for k in range(R + 1):
        rows = pl.ds(k * list_len, list_len)
        counts = tally_ref[...] if k == 0 else sizes_ref[k]
        grid_ref[3, rows, :tiles] = jnp.broadcast_to(counts, (list_len, tiles))
        for a in range(3):
            grid_ref[a, rows, :tiles] = lists_ref[k] if a == 0 else names_ref[a - 1, k]
    for a in range(3):
        counts = tally_ref[...] if a == 0 else sizes_ref[R + a]
        grid_ref[4 + a, :, :tiles] = jnp.broadcast_to(counts, (lines, tiles))
    row = lax.broadcasted_iota(jnp.int32, shape, 0)
    lane = lax.broadcasted_iota(jnp.int32, shape, 1)

    def spread(first):
        second = pltpu.roll(grid_ref[first + 1], tiles, 1)
        return grid_ref[first] + second + pltpu.roll(grid_ref[first + 2], 2 * tiles, 1)

    lower = (wall > 0).astype(jnp.int32)
    upper = (wall < walls - 1).astype(jnp.int32)
    open_lane = jnp.where(
        lane < tiles,
        1,
        jnp.where(lane < 2 * tiles, lower, jnp.where(lane < 3 * tiles, upper, 0)),
    )
    low = jnp.where(lane < tiles, tiles, jnp.where(lane < 2 * tiles, 2 * tiles, 0))
    near = spread(0) - low
    inside = jnp.logical_and(jnp.logical_and(near >= 0, near < tiles), open_lane > 0)
    inside = jnp.logical_and(inside, row < used)
    full = jnp.where(grid_ref[3] > LANES, 1, 0)
    wide = jnp.zeros(shape, jnp.int32)
    for b in range(tiles):
        wide = jnp.where(near == b, jnp.broadcast_to(full[:, b : b + 1], shape), wide)
    groups = lax.shift_right_logical(spread(4) + (ROWS - 1), SHIFT)
    kinds = 2 * top
    kind = jnp.where(inside, top - groups + (1 - wide) * top, -1)
    hits = jnp.concatenate([jnp.where(kind == c, 1.0, 0.0) for c in range(kinds)], axis=0)
    size = kinds * lines
    exact = None if max(3 * tiles, 2 * used * tiles) <= 512 else lax.Precision.HIGHEST

    def dot(left, right):
        if exact is None:
            left, right = left.astype(jnp.bfloat16), right.astype(jnp.bfloat16)
        return jnp.dot(left, right, preferred_element_type=jnp.float32, precision=exact)

    up = lax.broadcasted_iota(jnp.int32, (LANES, LANES), 0)
    across = lax.broadcasted_iota(jnp.int32, (LANES, LANES), 1)
    ahead = dot(hits, jnp.where(up <= across, 1.0, 0.0))
    sums = jnp.broadcast_to(ahead[:, LANES - 1 :], (size, LANES))
    down = lax.broadcasted_iota(jnp.int32, (size, size), 0)
    over = lax.broadcasted_iota(jnp.int32, (size, size), 1)
    home, away = down // lines, over // lines
    same = home == away
    before = dot(jnp.where(jnp.logical_and(same, over < down), 1.0, 0.0), sums)
    total = dot(jnp.where(same, 1.0, 0.0), sums)
    halves_of = lambda value: (jnp.floor(value * 0.5), value - 2.0 * jnp.floor(value * 0.5))
    pairs_of, odd_of = halves_of(total)
    first = jnp.where(jnp.logical_and(away < home, over == away * lines), 1.0, 0.0)
    start = dot(first, pairs_of) * 2.0 + dot(first, odd_of)
    heavy = start[top * lines : top * lines + 1]
    gap = heavy - 2.0 * jnp.floor(heavy * 0.5)
    start = start + jnp.where(down[:, :1] >= top * lines, gap, 0.0)
    spots = start + before + (ahead - hits)
    trash = float(3 * used * tiles + 16)
    place = jnp.full(shape, trash, jnp.float32)
    extra = jnp.full(shape, trash, jnp.float32)
    begin = jnp.zeros(shape, jnp.float32)
    for c in range(kinds):
        part = slice(c * lines, (c + 1) * lines)
        place = jnp.where(hits[part] > 0.0, spots[part], place)
        begin = jnp.where(lane == c, jnp.floor((start[part] + 1.0) * 0.5), begin)
    last = start[size - lines :] + total[size - lines :]
    begin = jnp.where(lane == kinds, jnp.floor((last + 1.0) * 0.5), begin)
    extra = jnp.where(lane == 0, jnp.where(gap > 0.0, heavy, trash), extra)
    for d in range(5):
        extra = jnp.where(lane == 1 + d, last + d, extra)
    at = near + lax.div(row, list_len) * tiles
    code = lax.shift_left(place.astype(jnp.int32), 16) + jnp.where(inside, at, 0)
    code = jnp.where(row == used, extra.astype(jnp.int32), code)
    codes_ref[...] = jnp.where(row == used + 1, begin.astype(jnp.int32), code)


def gather_kernel(
    chans,
    walls,
    coords_in,
    masses_in,
    tally_in,
    lists_in,
    ext_ref,
    over_out,
    codes_out,
    sizes_ref,
    names_ref,
    grid_ref,
    codes_ref,
    coords_ref,
    masses_ref,
    tally_ref,
    lists_ref,
    over_ref,
    own_ref,
    send_sem,
    recv_sem,
    pass_sem,
    size_send,
    size_recv,
    name_send,
    name_recv,
    local_sem,
):
    chan = lax.axis_index("chan")
    wall = lax.axis_index("wall")
    odd = lax.rem(chan, 2)
    twin = chan + 1 - 2 * odd
    sides = (wall > 0).astype(jnp.int32) + (wall < walls - 1).astype(jnp.int32)
    fetches = [
        pltpu.make_async_copy(source, target, local_sem.at[i])
        for i, (source, target) in enumerate(
            (
                (masses_in, masses_ref),
                (tally_in, tally_ref),
                (coords_in, coords_ref),
                (lists_in, lists_ref),
            )
        )
    ]
    for one in fetches:
        one.start()
    sizes_ref[...] = jnp.zeros_like(sizes_ref)
    names_ref[...] = jnp.zeros_like(names_ref)
    barrier = pltpu.get_barrier_semaphore()
    for k in range(1, R + 1):
        target = (lax.rem(chan + k, chans), wall)
        pl.semaphore_signal(barrier, inc=1, device_id=target, device_id_type=MESH)

    @pl.when(odd == 1)
    def _():
        pl.semaphore_signal(barrier, inc=1, device_id=(twin, wall), device_id_type=MESH)

    for _, other, there in wall_cases(wall, walls):
        @pl.when(there)
        def _(other=other):
            pl.semaphore_signal(barrier, inc=1, device_id=(chan, other), device_id_type=MESH)

    tiles, tile_len = over_ref.shape[1:]
    parts = tile_len // LANES
    height = tiles * parts

    def load(ref, base):
        return jnp.concatenate(
            [ref[pl.ds(base + h, tiles, stride=parts), :] for h in range(parts)], axis=1
        )

    spot = lax.broadcasted_iota(jnp.int32, (tiles, tile_len), 0)
    slot = lax.broadcasted_iota(jnp.int32, (tiles, tile_len), 1)
    for one in fetches:
        one.wait()
    tally = jnp.broadcast_to(tally_ref[...].astype(jnp.float32), (tiles, tiles))
    same = spot[:, :tiles] == slot[:, :tiles]
    limit = jnp.sum(jnp.where(same, tally, 0.0), axis=1, keepdims=True)
    filled = slot.astype(jnp.float32) < limit
    mass = load(masses_ref, 0)
    root = jnp.exp(jnp.log(mass) * (1.0 / 3.0))
    root = root - (root * root * root - mass) / (3.0 * root * root)
    over_ref[0] = jnp.where(filled, 1.0, 0.0)
    over_ref[1] = jnp.where(filled, 1.0 / mass, 0.0)
    fields = [load(coords_ref, i * height) for i in range(3)] + [jnp.where(filled, root, 0.0)]
    for i, field in enumerate(fields):
        for h in range(parts):
            own_ref[h, pl.ds(i, tiles, stride=4), :] = field[:, h * LANES : (h + 1) * LANES]

    keep = [
        pltpu.make_async_copy(own_ref, ext_ref.at[0], local_sem.at[0]),
        pltpu.make_async_copy(over_ref, over_out, local_sem.at[1]),
        pltpu.make_async_copy(codes_ref, codes_out, local_sem.at[2]),
    ]
    pl.semaphore_wait(barrier, R + 1 + sides - odd)

    def remote(source, target, sent, got, device):
        return pltpu.make_async_remote_copy(
            src_ref=source,
            dst_ref=target,
            send_sem=sent,
            recv_sem=got,
            device_id=device,
            device_id_type=MESH,
        )

    def behind(k):
        return (lax.rem(chan + chans - k, chans), wall)

    def copy(k):
        return remote(own_ref, ext_ref.at[k], send_sem.at[k], recv_sem.at[k], behind(k))

    def tell(k):
        return remote(tally_ref, sizes_ref.at[k], size_send.at[k], size_recv.at[k], behind(k))

    def aside(side, other, what):
        slab = R + 1 + side
        device = (chan, other)
        source, target, sent, got = (
            (own_ref, ext_ref.at[slab], send_sem.at[slab], recv_sem.at[slab]),
            (tally_ref, sizes_ref.at[slab], size_send.at[slab], size_recv.at[slab]),
            (lists_ref, names_ref.at[side], name_send.at[side], name_recv.at[side]),
        )[what]
        return remote(source, target, sent, got, device)

    def relay(k, own=False):
        into = k - 1 + 2 * odd
        source = own_ref if own else ext_ref.at[k]
        return remote(source, ext_ref.at[into], pass_sem.at[into], recv_sem.at[into], (twin, wall))

    for k in range(1, R + 1):
        tell(k).start()
    for side, other, there in wall_cases(wall, walls):
        @pl.when(there)
        def _(side=side, other=other):
            for what in (1, 2):
                aside(1 - side, other, what).start()

    copy(2).start()
    copy(4).start()
    for side, other, there in wall_cases(wall, walls):
        @pl.when(there)
        def _(side=side, other=other):
            aside(1 - side, other, 0).start()

    @pl.when(odd == 1)
    def _():
        relay(0, True).start()

    for one in keep[:2]:
        one.start()
    for k in range(1, R + 1):
        tell(k).wait()
    for side, other, there in wall_cases(wall, walls):
        @pl.when(there)
        def _(side=side, other=other):
            for what in (1, 2):
                aside(side, other, what).wait_recv()
                aside(1 - side, other, what).wait_send()

    arrange(wall, walls, tiles, tile_len, lists_ref, names_ref, tally_ref, sizes_ref, grid_ref, codes_ref)
    keep[2].start()

    @pl.when(odd == 0)
    def _():
        for k in (2, 4):
            copy(k).wait_recv()
            relay(k).start()

    @pl.when(odd == 1)
    def _():
        copy(2).wait_recv()
        relay(2).start()
        copy(4).wait_recv()

    for side, other, there in wall_cases(wall, walls):
        @pl.when(there)
        def _(side=side, other=other):
            aside(side, other, 0).wait_recv()
            aside(1 - side, other, 0).wait_send()

    copy(1).wait_recv()
    copy(3).wait_recv()
    copy(2).wait_send()
    copy(4).wait_send()

    @pl.when(odd == 0)
    def _():
        relay(2).wait_send()
        relay(4).wait_send()

    @pl.when(odd == 1)
    def _():
        relay(0, True).wait_send()
        relay(2).wait_send()

    for one in keep:
        one.wait()


def gather(coords, masses, counts, lists, chans, walls):
    slabs = R + 3
    tiles = counts.shape[0]
    tile_len = masses.shape[0] * LANES // tiles
    hbm = pl.BlockSpec(memory_space=pl.ANY)
    block = (tile_len // LANES, 4 * tiles, LANES)
    tally = counts.reshape(1, tiles)
    lines = -(-((R + 1) * lists.shape[1] + 2) // 8) * 8
    many = pltpu.SemaphoreType.DMA((slabs,))
    few = pltpu.SemaphoreType.DMA((2,))
    return pl.pallas_call(
        functools.partial(gather_kernel, chans, walls),
        out_shape=(
            jax.ShapeDtypeStruct((slabs,) + block, jnp.float32),
            jax.ShapeDtypeStruct((2, tiles, tile_len), jnp.float32),
            jax.ShapeDtypeStruct((lines, LANES), jnp.int32),
        ),
        in_specs=[hbm] * 4,
        out_specs=(hbm,) * 3,
        scratch_shapes=[
            pltpu.VMEM((slabs,) + tally.shape, jnp.int32),
            pltpu.VMEM((2,) + lists.shape, jnp.int32),
            pltpu.VMEM((7, lines, LANES), jnp.int32),
            pltpu.VMEM((lines, LANES), jnp.int32),
            pltpu.VMEM(coords.shape, jnp.float32),
            pltpu.VMEM(masses.shape, jnp.float32),
            pltpu.VMEM(tally.shape, jnp.int32),
            pltpu.VMEM(lists.shape, jnp.int32),
            pltpu.VMEM((2, tiles, tile_len), jnp.float32),
            pltpu.VMEM(block, jnp.float32),
            many,
            many,
            many,
            many,
            many,
            few,
            few,
            pltpu.SemaphoreType.DMA((4,)),
        ],
        compiler_params=pltpu.CompilerParams(collective_id=0, has_side_effects=True),
    )(coords, masses, tally, lists)


def splits(v):
    first = v.astype(jnp.bfloat16).astype(jnp.float32)
    rest = v - first
    second = rest.astype(jnp.bfloat16).astype(jnp.float32)
    third = (rest - second).astype(jnp.bfloat16).astype(jnp.float32)
    return first, second, third


def halves(block, row):
    low = jnp.broadcast_to(block[row : row + 1], block.shape)
    high = jnp.broadcast_to(block[row + 4 : row + 5], block.shape)
    spot = lax.broadcasted_iota(jnp.int32, block.shape, 0)
    return low, high, jnp.where(spot < 4, low, high)


def pair_kernel(
    walls,
    codes_in,
    far_ref,
    gained_ref,
    handed_ref,
    afeat,
    wcol,
    bfeat,
    brow,
    gacc,
    hands,
    codes,
    items,
    ext_ref,
    load_sem,
    code_sem,
):
    _, tiles, tile_len = gained_ref.shape
    slots = (R + 1) * tiles
    parts = tile_len // LANES
    wall = lax.axis_index("wall")
    near = ((0, wall > 0), (1, wall < walls - 1))
    slabs = far_ref.shape[0]

    def bring(at):
        return pltpu.make_async_copy(far_ref.at[at], ext_ref.at[at], load_sem.at[at])

    decode = pltpu.make_async_copy(codes_in, codes, code_sem)
    bring(0).start()
    decode.start()
    for side, there in near:
        pl.when(there)(lambda side=side: bring(R + 1 + side).start())
    for k in range(1, R + 1):
        bring(k).start()
    classes = 2 * (tile_len // ROWS)
    used = (R + 1) * NB

    def block_of(slab, i):
        rows = pl.ds(pl.multiple_of(i * 8, 8), 8)
        return jnp.concatenate([ext_ref[slab, h, rows, :] for h in range(parts)], axis=1)

    spot = lax.broadcasted_iota(jnp.int32, (8, tile_len), 0)
    part = jnp.bitwise_and(spot, 3)
    quarter = 1.0 / R
    base = jnp.where(part == 0, -0.5, jnp.where(part == 3, 0.0, -float(R))) * quarter
    scale = jnp.where(part == 3, 1.0, quarter)

    def own_pair(i, a):
        block = block_of((0, R + 1, R + 2)[a], i)
        _, _, s = halves(block, 3)
        lift = jnp.where(part == 1, (0.0, -2.0, 2.0)[a], 0.0)
        place = jnp.where(part == 3, 0.0, block * scale + (base + lift))
        square = place * place
        pairsum = square + pltpu.roll(square, 1, 0)
        total = pairsum + pltpu.roll(pairsum, 2, 0)
        full = jnp.where(part == 3, total, place)
        one, two, three = splits(full)
        ones = jnp.where(part == 3, 1.0, 0.0)
        weight = s * s * s
        rest = jnp.zeros((LANES - 80, tile_len), jnp.float32)
        stack = jnp.concatenate(
            [one, one, two, two, one, three, ones, ones, ones, weight, rest], axis=0
        )
        turned = jnp.transpose(stack, (1, 0))
        lane = lax.broadcasted_iota(jnp.int32, turned.shape, 1)
        low = jnp.bitwise_and(lane, 4) == 0
        inside = lane < 72
        for half in range(2):
            t = 2 * i + half + a * tiles
            keep = low if half == 0 else jnp.logical_not(low)
            mine = jnp.where(jnp.logical_and(keep, inside), turned, 0.0)
            other = pltpu.roll(mine, 4 if half == 0 else LANES - 4, 1)
            afeat[half * 3 * tiles + t] = mine.astype(jnp.bfloat16)
            afeat[(1 - half) * 3 * tiles + t] = other.astype(jnp.bfloat16)
            wcol[t] = jnp.broadcast_to(
                turned[:, 72 + 4 * half : 73 + 4 * half], (tile_len, LANES)
            )

    def enlist(t, a):
        spot = t + a * tiles
        high_bits = lax.shift_left(spot, 16)
        for r in range(used):
            code = codes[r, spot]
            items[lax.shift_right_logical(code, 16)] = high_bits + jnp.bitwise_and(code, 65535)

    def prepare(a):
        bring((0, R + 1, R + 2)[a]).wait()

        def pair_of(i, carry):
            enlist(2 * i, a)
            enlist(2 * i + 1, a)
            own_pair(i, a)
            return carry

        lax.fori_loop(0, tiles // 2, pair_of, 0)

    hands[...] = jnp.zeros_like(hands)

    def clear(t, carry):
        gacc[t] = jnp.zeros((tile_len, LANES), jnp.float32)
        return carry

    lax.fori_loop(0, 3 * tiles, clear, 0)
    decode.wait()
    prepare(0)
    for side, there in near:
        pl.when(there)(functools.partial(prepare, side + 1))
    for k in range(1, R + 1):
        bring(k).wait()

    def ext_pair(i, k):
        at = k * (tiles // 2) + i
        block = block_of(k, i)
        low, high, s = halves(block, 3)
        filled = s > 0.0
        place = block * scale + (base + jnp.where(part == 0, k * quarter, 0.0))
        place = jnp.where(jnp.logical_and(part < 3, filled), place, 0.0)
        s = jnp.where(filled, s, 1.0)
        s2 = s * s
        square = place * place
        pairsum = square + pltpu.roll(square, 1, 0)
        total = pairsum + pltpu.roll(pairsum, 2, 0)
        tail = jnp.where(filled, s2 * (total + 0.0001 / (R * R)), 128.0)
        full = jnp.where(part == 3, s2, -2.0 * s2 * place)
        one, two, three = splits(full)
        first, second, third = splits(tail)
        stack = jnp.concatenate(
            [one, two, one, two, three, one, first, second, third, jnp.zeros_like(one)],
            axis=0,
        )
        bfeat[at] = stack.astype(jnp.bfloat16)
        for half, root in enumerate((low, high)):
            root = jnp.where(root > 0.0, root, 1.0)
            brow[at * 2 + half, :8] = 2.0 * root
            brow[at * 2 + half, 8:] = 4.0 * root * root * root

    def ext_pairs(i, carry):
        for k in range(R + 1):
            ext_pair(i, k)
        return carry

    lax.fori_loop(0, tiles // 2, ext_pairs, 0)
    nothing = ((3 * tiles) << 16) + slots
    for c in range(6):
        items[codes[used, c]] = nothing
    ends = [codes[used + 1, c] for c in range(classes + 1)]

    def body(*accs):
        pieces = tile_len // PIECE
        for ref in accs:
            pltpu.matmul_pop(ref)

        def fields(m):
            packed = items[m]
            at = jnp.bitwise_and(packed, 65535)
            return at, lax.shift_right_logical(packed, 16)

        def push(m, q):
            at, _ = fields(m)
            rhs = jnp.concatenate(
                [
                    bfeat[lax.shift_right_logical(at, 1)],
                    jnp.zeros((256 - 80, tile_len), jnp.bfloat16),
                ],
                axis=0,
            )
            pltpu.matmul_push_rhs(rhs, staging_register=0, mxu_index=q)

        def feed(which, q, p):
            lhs = afeat[which, p * PIECE : (p + 1) * PIECE]
            lhs = jnp.concatenate([lhs, jnp.zeros((PIECE, 256 - LANES), jnp.bfloat16)], axis=1)
            pltpu.matmul_acc_lhs(
                accs[q * pieces + p], lhs, load_staged_rhs=0 if p == 0 else None
            )

        def which_of(m):
            at, t = fields(m)
            return jnp.bitwise_and(at, 1) * (3 * tiles) + t

        def run(j, carry, groups, width):
            now = [fields(2 * j + q) for q in range(2)]
            then = [which_of(2 * j + 2 + q) for q in range(2)]
            rows = [
                [brow[at, r * 8 : r * 8 + 8, h * LANES : (h + 1) * LANES] for r in range(2) for h in range(width)]
                for at, _ in now
            ]
            sums = [[None] * width for _ in now]
            for p in range(pieces if width > 1 else groups * ROWS // PIECE):
                for q, (at, t) in enumerate(now):
                    u = pltpu.matmul_pop(accs[q * pieces + p])
                    feed(then[q], q, p)
                    if p == 0:
                        push(2 * j + 4 + q, q)
                    if p >= groups * ROWS // PIECE:
                        continue
                    for r in range(0, PIECE, 8):
                        here = pl.ds(p * PIECE + r, 8)
                        aw = wcol[t, here, :]
                        total = None
                        for h in range(width):
                            v = u[r : r + 8, h * LANES : (h + 1) * LANES]
                            o = jnp.maximum(rows[q][h] - v * lax.rsqrt(v), 0.0)
                            w = jnp.minimum(o * o * o, rows[q][width + h] - (v * o) * 3.0)
                            total = w if total is None else total + w
                            back = w * aw
                            sums[q][h] = back if sums[q][h] is None else sums[q][h] + back
                        gacc[t, here, :] += total
            for q, (at, t) in enumerate(now):
                for h in range(width):
                    hands[at, :, h * LANES : (h + 1) * LANES] += sums[q][h]
            return carry

        for q in range(2):
            push(q, q)
        for q in range(2):
            for p in range(pieces):
                feed(which_of(q), q, p)
        for q in range(2):
            push(2 + q, q)
        for c in range(classes):
            top = classes // 2
            lax.fori_loop(
                ends[c],
                ends[c + 1],
                functools.partial(run, groups=top - c % top, width=2 - c // top),
                0,
            )
        for q in range(2):
            for p in range(pieces):
                feed(which_of(q), q, p)
        for ref in accs:
            pltpu.matmul_pop(ref)

    pl.run_scoped(
        body,
        *[pltpu.ACC(q)((PIECE, 256), jnp.float32) for q in range(2) for _ in range(tile_len // PIECE)],
    )
    lane = lax.broadcasted_iota(jnp.int32, (tile_len, LANES), 1)

    def finish(a):
        columns = jnp.zeros((tile_len, LANES), jnp.float32)
        for t in range(tiles):
            value = jnp.sum(gacc[a * tiles + t], axis=1, keepdims=True)
            columns = jnp.where(lane == t, value, columns)
        gained_ref[a] = jnp.transpose(columns, (1, 0))[:tiles]

    finish(0)
    for side, there in near:
        pl.when(there)(functools.partial(finish, side + 1))
    handed_ref[...] = jnp.sum(hands[tiles:slots], axis=1).reshape(handed_ref.shape)


def pairs(codes, ext, walls):
    tiles = ext.shape[2] // 4
    tile_len = ext.shape[1] * LANES
    hbm = pl.BlockSpec(memory_space=pl.ANY)
    vmem = pl.BlockSpec(memory_space=pltpu.VMEM)
    slots = (R + 1) * tiles
    entries = 3 * slots * NB
    return pl.pallas_call(
        functools.partial(pair_kernel, walls),
        out_shape=(
            jax.ShapeDtypeStruct((3, tiles, tile_len), jnp.float32),
            jax.ShapeDtypeStruct((R, tiles, tile_len), jnp.float32),
        ),
        in_specs=[hbm, hbm],
        out_specs=(vmem, vmem),
        scratch_shapes=[
            pltpu.VMEM((6 * tiles, tile_len, LANES), jnp.bfloat16),
            pltpu.VMEM((3 * tiles + 1, tile_len, LANES), jnp.float32),
            pltpu.VMEM((slots // 2 + 1, 80, tile_len), jnp.bfloat16),
            pltpu.VMEM((slots + 1, 16, tile_len), jnp.float32),
            pltpu.VMEM((3 * tiles + 1, tile_len, LANES), jnp.float32),
            pltpu.VMEM((slots + 1, 8, tile_len), jnp.float32),
            pltpu.SMEM(codes.shape, jnp.int32),
            pltpu.SMEM((entries + 32,), jnp.int32),
            pltpu.VMEM(ext.shape, jnp.float32),
            pltpu.SemaphoreType.DMA((ext.shape[0],)),
            pltpu.SemaphoreType.DMA,
        ],
    )(codes, ext)


def return_kernel(
    chans,
    walls,
    gained_in,
    handed_in,
    over_in,
    out_ref,
    gained_ref,
    handed_ref,
    over_ref,
    held,
    hold,
    send_sem,
    recv_sem,
    local_sem,
):
    chan = lax.axis_index("chan")
    wall = lax.axis_index("wall")
    sides = (wall > 0).astype(jnp.int32) + (wall < walls - 1).astype(jnp.int32)
    pulls = [
        pltpu.make_async_copy(source, target, local_sem.at[i])
        for i, (source, target) in enumerate(
            ((handed_in, handed_ref), (gained_in, gained_ref), (over_in, over_ref))
        )
    ]
    for one in pulls:
        one.start()
    barrier = pltpu.get_barrier_semaphore()
    for k in range(1, R + 1):
        target = (lax.rem(chan + chans - k, chans), wall)
        pl.semaphore_signal(barrier, inc=1, device_id=target, device_id_type=MESH)
    for _, other, there in wall_cases(wall, walls):
        @pl.when(there)
        def _(other=other):
            pl.semaphore_signal(barrier, inc=1, device_id=(chan, other), device_id_type=MESH)
    for one in pulls:
        one.wait()
    pl.semaphore_wait(barrier, R + sides)

    def copy(source, slot, device):
        return pltpu.make_async_remote_copy(
            src_ref=source,
            dst_ref=held.at[slot],
            send_sem=send_sem.at[slot],
            recv_sem=recv_sem.at[slot],
            device_id=device,
            device_id_type=MESH,
        )

    def ahead(k):
        return copy(handed_ref.at[k - 1], k - 1, (lax.rem(chan + k, chans), wall))

    def aside(side, slot, other):
        return copy(gained_ref.at[side + 1], R + slot, (chan, other))

    for k in range(R, 0, -1):
        ahead(k).start()
    for side, other, there in wall_cases(wall, walls):
        @pl.when(there)
        def _(side=side, other=other):
            aside(side, 1 - side, other).start()

    tiles = hold.shape[0]
    hold[...] = gained_ref[0]
    for side, other, there in wall_cases(wall, walls):
        @pl.when(there)
        def _(side=side, other=other):
            aside(side, side, other).wait_recv()
            hold[...] += held[R + side]

    handed = None
    for k in range(1, R + 1):
        ahead(k).wait_recv()
        handed = held[k - 1] if handed is None else handed + held[k - 1]
    total = hold[...] * over_ref[0] + handed * over_ref[1]
    parts = hold.shape[1] // LANES
    for h in range(parts):
        out_ref[pl.ds(h, tiles, stride=parts), :] = total[:, h * LANES : (h + 1) * LANES]
    for k in range(1, R + 1):
        ahead(k).wait_send()
    for side, other, there in wall_cases(wall, walls):
        @pl.when(there)
        def _(side=side, other=other):
            aside(side, 1 - side, other).wait_send()


def hand_back(gained, handed, over, chans, walls):
    _, tiles, tile_len = gained.shape
    vmem = pl.BlockSpec(memory_space=pltpu.VMEM)
    return pl.pallas_call(
        functools.partial(return_kernel, chans, walls),
        out_shape=jax.ShapeDtypeStruct((tiles * tile_len // LANES, LANES), gained.dtype),
        in_specs=[pl.BlockSpec(memory_space=pl.ANY)] * 3,
        out_specs=vmem,
        scratch_shapes=[
            pltpu.VMEM(gained.shape, jnp.float32),
            pltpu.VMEM(handed.shape, jnp.float32),
            pltpu.VMEM(over.shape, jnp.float32),
            pltpu.VMEM((R + 2, tiles, tile_len), jnp.float32),
            pltpu.VMEM((tiles, tile_len), jnp.float32),
            pltpu.SemaphoreType.DMA((R + 2,)),
            pltpu.SemaphoreType.DMA((R + 2,)),
            pltpu.SemaphoreType.DMA((3,)),
        ],
        compiler_params=pltpu.CompilerParams(collective_id=1, has_side_effects=True),
    )(gained, handed, over)


def on_device(chans, walls, coords, masses, counts, lists):
    tiles = counts.shape[2]
    tile_len = masses.shape[2] // tiles
    scale = 1.0 / (4.0 * math.pi * NB * tile_len)
    lists = jnp.swapaxes(lists.reshape(lists.shape[2:]), 1, 2)
    ext, over, codes = gather(
        coords.reshape(-1, LANES),
        masses.reshape(-1, LANES),
        counts.reshape(-1),
        lists,
        chans,
        walls,
    )
    gained, handed = pairs(codes, ext, walls)
    total = hand_back(gained, handed, over, chans, walls)
    return total.reshape(1, 1, -1) * scale


def solution(mesh):
    placed = (
        P(None, "chan", "wall", None),
        P("chan", "wall", None),
        P("chan", "wall", None),
        P("chan", "wall", None, None, None),
    )
    body = functools.partial(on_device, mesh.shape["chan"], mesh.shape["wall"])
    return jax.shard_map(
        body, mesh=mesh, in_specs=placed, out_specs=P("chan", "wall", None), check_vma=False
    )
```

profile of v0, /device:TPU:0, one launch (start us, length us, event | category | flops | bytes accessed | tf_op | source)
XLA Modules:
  0.0 40.8 jit_solution(17987392713182225498)
XLA Ops:
  0.0 11.7 %shard_map.46 = (f32[7,2,64,128]{3,2,1,0:T(8,128)}, f32[2,16,256]{2,1,0:T(8,128)}, s32[16,128]{1,0:T(8,128)}) custom-call(f32[96,128]{1,0:T(8,128)} %bitcast.7, f32[32,128]{1,0:T(8,128)} %bitcast.8, s32[1,16]{1,0:T(1,128)} %bitcast.10, s32[5,2,16]{2,1,0:T(2,128)} %bitcast.9), custom_call_target="tpu_custom_call" | custom-call | tf_op jit(solution)/shard_map/pallas_call | solution.py:324
  11.7 17.9 %shard_map.47 = (f32[3,16,256]{2,1,0:T(8,128)}, f32[4,16,256]{2,1,0:T(8,128)}) custom-call(s32[16,128]{1,0:T(8,128)} %get-tuple-element.10.codes_in, f32[7,2,64,128]{3,2,1,0:T(8,128)} %get-tuple-element.11.far_ref), custom_call_target="tpu_custom_call" | custom-call | tf_op jit(solution)/shard_map/pallas_call | solution.py:632
  29.6 9.9 %shard_map.48 = f32[32,128]{1,0:T(8,128)} custom-call(f32[3,16,256]{2,1,0:T(8,128)} %get-tuple-element.12.gained_in, f32[4,16,256]{2,1,0:T(8,128)} %get-tuple-element.13.handed_in, f32[2,16,256]{2,1,0:T(8,128)} %get-tuple-element.14.over_in), custom_call_target="tpu_custom_call" | custom-call | tf_op jit(solution)/shard_map/pallas_call | solution.py:745
  39.5 1.3 %broadcast_multiply_fusion = f32[32,128]{1,0:T(8,128)} fusion(f32[32,128]{1,0:T(8,128)} %shard_map.48), kind=kLoop, calls=%fused_computation | loop fusion | flops 4096 | bytes 32768 | tf_op jit(solution)/shard_map/mul | solution.py:779
where the time goes:
time: 40.5 us; the launch traced here: 40.8 us
  Pallas kernels  39.5 us (98%)
  other arithmetic  1.33 us (3%)
    pallas_call x1, Pallas kernels, pairs(): pl.pallas_call(functools.partial(pair_kernel, walls), out_shape=(jax.Shap...  17.9 us
    pallas_call x1, Pallas kernels, gather(): pl.pallas_call(functools.partial(gather_kernel, chans, walls), out_shape=...  11.7 us
    pallas_call x1, Pallas kernels, hand_back(): pl.pallas_call(functools.partial(return_kernel, chans, walls), out_shape=...  9.93 us
    mul x1, other arithmetic, on_device(): return total.reshape(1, 1, -1) * scale  1.33 us

commit v1 on v0

--- a/solution.py
+++ b/solution.py
@@ -417,7 +417,7 @@
     base = jnp.where(part == 0, -0.5, jnp.where(part == 3, 0.0, -float(R))) * quarter
     scale = jnp.where(part == 3, 1.0, quarter)
 
-    def own_pair(i, a):
+    def own_pair(i, a, accs, past):
         block = block_of((0, R + 1, R + 2)[a], i)
         _, _, s = halves(block, 3)
         lift = jnp.where(part == 1, (0.0, -2.0, 2.0)[a], 0.0)
@@ -428,25 +428,35 @@
         full = jnp.where(part == 3, total, place)
         one, two, three = splits(full)
         ones = jnp.where(part == 3, 1.0, 0.0)
-        weight = s * s * s
-        rest = jnp.zeros((LANES - 80, tile_len), jnp.float32)
+        weight = splits(s * s * s)
+        rest = jnp.zeros((LANES - 96, tile_len), jnp.float32)
         stack = jnp.concatenate(
-            [one, one, two, two, one, three, ones, ones, ones, weight, rest], axis=0
+            [one, one, two, two, one, three, ones, ones, ones, *weight, rest], axis=0
         )
         turned = jnp.transpose(stack, (1, 0))
         lane = lax.broadcasted_iota(jnp.int32, turned.shape, 1)
         low = jnp.bitwise_and(lane, 4) == 0
-        inside = lane < 72
         for half in range(2):
             t = 2 * i + half + a * tiles
             keep = low if half == 0 else jnp.logical_not(low)
-            mine = jnp.where(jnp.logical_and(keep, inside), turned, 0.0)
+            mine = jnp.where(keep, turned, 0.0)
             other = pltpu.roll(mine, 4 if half == 0 else LANES - 4, 1)
             afeat[half * 3 * tiles + t] = mine.astype(jnp.bfloat16)
             afeat[(1 - half) * 3 * tiles + t] = other.astype(jnp.bfloat16)
-            wcol[t] = jnp.broadcast_to(
-                turned[:, 72 + 4 * half : 73 + 4 * half], (tile_len, LANES)
-            )
+        drain(accs, past)
+        whole = jnp.concatenate(
+            [turned.astype(jnp.bfloat16), jnp.zeros((tile_len, 256 - LANES), jnp.bfloat16)], axis=1
+        )
+        for p in range(tile_len // PIECE):
+            pltpu.matmul_acc_lhs(accs[p], whole[p * PIECE : (p + 1) * PIECE])
+
+    def drain(accs, past):
+        for p in range(tile_len // PIECE):
+            value = pltpu.matmul_pop(accs[p])
+            for half in range(2):
+                wcol[past[half], p * PIECE : (p + 1) * PIECE, :] = value[
+                    :, half * LANES : (half + 1) * LANES
+                ]
 
     def enlist(t, a):
         spot = t + a * tiles
@@ -455,16 +465,17 @@
             code = codes[r, spot]
             items[lax.shift_right_logical(code, 16)] = high_bits + jnp.bitwise_and(code, 65535)
 
-    def prepare(a):
+    def prepare(a, accs):
         bring((0, R + 1, R + 2)[a]).wait()
 
-        def pair_of(i, carry):
+        def pair_of(i, past):
             enlist(2 * i, a)
             enlist(2 * i + 1, a)
-            own_pair(i, a)
-            return carry
-
-        lax.fori_loop(0, tiles // 2, pair_of, 0)
+            own_pair(i, a, accs, past)
+            return 2 * i + a * tiles, 2 * i + 1 + a * tiles
+
+        nowhere = jnp.int32(3 * tiles)
+        drain(accs, lax.fori_loop(0, tiles // 2, pair_of, (nowhere, nowhere), unroll=4))
 
     hands[...] = jnp.zeros_like(hands)
 
@@ -474,53 +485,75 @@
 
     lax.fori_loop(0, 3 * tiles, clear, 0)
     decode.wait()
-    prepare(0)
-    for side, there in near:
-        pl.when(there)(functools.partial(prepare, side + 1))
-    for k in range(1, R + 1):
-        bring(k).wait()
-
-    def ext_pair(i, k):
-        at = k * (tiles // 2) + i
-        block = block_of(k, i)
-        low, high, s = halves(block, 3)
-        filled = s > 0.0
-        place = block * scale + (base + jnp.where(part == 0, k * quarter, 0.0))
-        place = jnp.where(jnp.logical_and(part < 3, filled), place, 0.0)
-        s = jnp.where(filled, s, 1.0)
-        s2 = s * s
-        square = place * place
-        pairsum = square + pltpu.roll(square, 1, 0)
-        total = pairsum + pltpu.roll(pairsum, 2, 0)
-        tail = jnp.where(filled, s2 * (total + 0.0001 / (R * R)), 128.0)
-        full = jnp.where(part == 3, s2, -2.0 * s2 * place)
-        one, two, three = splits(full)
-        first, second, third = splits(tail)
-        stack = jnp.concatenate(
-            [one, two, one, two, three, one, first, second, third, jnp.zeros_like(one)],
+
+    def outset(*accs):
+        for ref in accs:
+            pltpu.matmul_pop(ref)
+        line = lax.broadcasted_iota(jnp.int32, (32, 256), 0)
+        spread = lax.broadcasted_iota(jnp.int32, (32, 256), 1)
+        wanted = jnp.bitwise_and(line, 7) == jnp.where(spread < LANES, 3, 7)
+        wanted = jnp.logical_and(wanted, line >= 8)
+        rhs = jnp.concatenate(
+            [
+                jnp.zeros((64, 256), jnp.bfloat16),
+                jnp.where(wanted, 1.0, 0.0).astype(jnp.bfloat16),
+                jnp.zeros((160, 256), jnp.bfloat16),
+            ],
             axis=0,
         )
-        bfeat[at] = stack.astype(jnp.bfloat16)
-        for half, root in enumerate((low, high)):
-            root = jnp.where(root > 0.0, root, 1.0)
-            brow[at * 2 + half, :8] = 2.0 * root
-            brow[at * 2 + half, 8:] = 4.0 * root * root * root
-
-    def ext_pairs(i, carry):
-        for k in range(R + 1):
-            ext_pair(i, k)
-        return carry
-
-    lax.fori_loop(0, tiles // 2, ext_pairs, 0)
-    nothing = ((3 * tiles) << 16) + slots
-    for c in range(6):
-        items[codes[used, c]] = nothing
-    ends = [codes[used + 1, c] for c in range(classes + 1)]
-
-    def body(*accs):
+        pltpu.matmul_push_rhs(rhs, staging_register=0, mxu_index=0)
+        pltpu.matmul_acc_lhs(
+            accs[0], jnp.zeros((PIECE, 256), jnp.bfloat16), load_staged_rhs=0
+        )
+        prepare(0, accs)
+        for side, there in near:
+            pl.when(there)(functools.partial(prepare, side + 1, accs))
+        rest_of(*accs)
+
+    def rest_of(*accs):
+        for k in range(1, R + 1):
+            bring(k).wait()
+
+        def ext_pair(i, k):
+            at = k * (tiles // 2) + i
+            block = block_of(k, i)
+            low, high, s = halves(block, 3)
+            filled = s > 0.0
+            place = block * scale + (base + jnp.where(part == 0, k * quarter, 0.0))
+            place = jnp.where(jnp.logical_and(part < 3, filled), place, 0.0)
+            s = jnp.where(filled, s, 1.0)
+            s2 = s * s
+            square = place * place
+            pairsum = square + pltpu.roll(square, 1, 0)
+            total = pairsum + pltpu.roll(pairsum, 2, 0)
+            tail = jnp.where(filled, s2 * (total + 0.0001 / (R * R)), 128.0)
+            full = jnp.where(part == 3, s2, -2.0 * s2 * place)
+            one, two, three = splits(full)
+            first, second, third = splits(tail)
+            stack = jnp.concatenate(
+                [one, two, one, two, three, one, first, second, third, jnp.zeros_like(one)],
+                axis=0,
+            )
+            bfeat[at] = stack.astype(jnp.bfloat16)
+            for half, root in enumerate((low, high)):
+                root = jnp.where(root > 0.0, root, 1.0)
+                brow[at * 2 + half, :8] = 2.0 * root
+                brow[at * 2 + half, 8:] = 4.0 * root * root * root
+
+        def ext_pairs(i, carry):
+            for k in range(R + 1):
+                ext_pair(i, k)
+            return carry
+
+        lax.fori_loop(0, tiles // 2, ext_pairs, 0, unroll=2)
+        nothing = ((3 * tiles) << 16) + slots
+        for c in range(6):
+            items[codes[used, c]] = nothing
+        ends = [codes[used + 1, c] for c in range(classes + 1)]
+        body(ends, *accs)
+
+    def body(ends, *accs):
         pieces = tile_len // PIECE
-        for ref in accs:
-            pltpu.matmul_pop(ref)
 
         def fields(m):
             packed = items[m]
@@ -604,7 +637,7 @@
             pltpu.matmul_pop(ref)
 
     pl.run_scoped(
-        body,
+        outset,
         *[pltpu.ACC(q)((PIECE, 256), jnp.float32) for q in range(2) for _ in range(tile_len // PIECE)],
     )
     lane = lax.broadcasted_iota(jnp.int32, (tile_len, LANES), 1)
@@ -658,13 +691,9 @@
     walls,
     gained_in,
     handed_in,
-    over_in,
-    out_ref,
+    held,
     gained_ref,
     handed_ref,
-    over_ref,
-    held,
-    hold,
     send_sem,
     recv_sem,
     local_sem,
@@ -672,12 +701,10 @@
     chan = lax.axis_index("chan")
     wall = lax.axis_index("wall")
     sides = (wall > 0).astype(jnp.int32) + (wall < walls - 1).astype(jnp.int32)
-    pulls = [
-        pltpu.make_async_copy(source, target, local_sem.at[i])
-        for i, (source, target) in enumerate(
-            ((handed_in, handed_ref), (gained_in, gained_ref), (over_in, over_ref))
-        )
-    ]
+    pulls = (
+        pltpu.make_async_copy(handed_in, handed_ref, local_sem.at[0]),
+        pltpu.make_async_copy(gained_in.at[pl.ds(1, 2)], gained_ref, local_sem.at[1]),
+    )
     for one in pulls:
         one.start()
     barrier = pltpu.get_barrier_semaphore()
@@ -706,7 +733,7 @@
         return copy(handed_ref.at[k - 1], k - 1, (lax.rem(chan + k, chans), wall))
 
     def aside(side, slot, other):
-        return copy(gained_ref.at[side + 1], R + slot, (chan, other))
+        return copy(gained_ref.at[side], R + slot, (chan, other))
 
     for k in range(R, 0, -1):
         ahead(k).start()
@@ -715,50 +742,60 @@
         def _(side=side, other=other):
             aside(side, 1 - side, other).start()
 
-    tiles = hold.shape[0]
-    hold[...] = gained_ref[0]
+    for k in range(1, R + 1):
+        ahead(k).wait()
     for side, other, there in wall_cases(wall, walls):
         @pl.when(there)
         def _(side=side, other=other):
             aside(side, side, other).wait_recv()
-            hold[...] += held[R + side]
-
-    handed = None
-    for k in range(1, R + 1):
-        ahead(k).wait_recv()
-        handed = held[k - 1] if handed is None else handed + held[k - 1]
-    total = hold[...] * over_ref[0] + handed * over_ref[1]
-    parts = hold.shape[1] // LANES
+            aside(side, 1 - side, other).wait_send()
+
+
+def hand_back(gained, handed, chans, walls):
+    _, tiles, tile_len = gained.shape
+    hbm = pl.BlockSpec(memory_space=pl.ANY)
+    return pl.pallas_call(
+        functools.partial(return_kernel, chans, walls),
+        out_shape=jax.ShapeDtypeStruct((R + 2, tiles, tile_len), jnp.float32),
+        in_specs=[hbm] * 2,
+        out_specs=hbm,
+        scratch_shapes=[
+            pltpu.VMEM((2, tiles, tile_len), jnp.float32),
+            pltpu.VMEM(handed.shape, jnp.float32),
+            pltpu.SemaphoreType.DMA((R + 2,)),
+            pltpu.SemaphoreType.DMA((R + 2,)),
+            pltpu.SemaphoreType.DMA((2,)),
+        ],
+        compiler_params=pltpu.CompilerParams(collective_id=1, has_side_effects=True),
+    )(gained, handed)
+
+
+def total_kernel(walls, scale, gained_ref, held_ref, over_ref, out_ref):
+    wall = lax.axis_index("wall")
+    _, tiles, tile_len = gained_ref.shape
+    parts = tile_len // LANES
+    total = gained_ref[0]
+    total += jnp.where(wall > 0, held_ref[R], 0.0)
+    total += jnp.where(wall < walls - 1, held_ref[R + 1], 0.0)
+    handed = held_ref[0]
+    for k in range(1, R):
+        handed += held_ref[k]
+    total = (total * over_ref[0] + handed * over_ref[1]) * scale
     for h in range(parts):
         out_ref[pl.ds(h, tiles, stride=parts), :] = total[:, h * LANES : (h + 1) * LANES]
-    for k in range(1, R + 1):
-        ahead(k).wait_send()
-    for side, other, there in wall_cases(wall, walls):
-        @pl.when(there)
-        def _(side=side, other=other):
-            aside(side, 1 - side, other).wait_send()
-
-
-def hand_back(gained, handed, over, chans, walls):
+
+
+def add_up(gained, held, over, scale, walls):
     _, tiles, tile_len = gained.shape
     vmem = pl.BlockSpec(memory_space=pltpu.VMEM)
+    first = pl.BlockSpec((1, tiles, tile_len), lambda i: (0, 0, 0))
     return pl.pallas_call(
-        functools.partial(return_kernel, chans, walls),
+        functools.partial(total_kernel, walls, scale),
+        grid=(1,),
         out_shape=jax.ShapeDtypeStruct((tiles * tile_len // LANES, LANES), gained.dtype),
-        in_specs=[pl.BlockSpec(memory_space=pl.ANY)] * 3,
+        in_specs=[first, vmem, vmem],
         out_specs=vmem,
-        scratch_shapes=[
-            pltpu.VMEM(gained.shape, jnp.float32),
-            pltpu.VMEM(handed.shape, jnp.float32),
-            pltpu.VMEM(over.shape, jnp.float32),
-            pltpu.VMEM((R + 2, tiles, tile_len), jnp.float32),
-            pltpu.VMEM((tiles, tile_len), jnp.float32),
-            pltpu.SemaphoreType.DMA((R + 2,)),
-            pltpu.SemaphoreType.DMA((R + 2,)),
-            pltpu.SemaphoreType.DMA((3,)),
-        ],
-        compiler_params=pltpu.CompilerParams(collective_id=1, has_side_effects=True),
-    )(gained, handed, over)
+    )(gained, held, over)
 
 
 def on_device(chans, walls, coords, masses, counts, lists):
@@ -775,8 +812,8 @@
         walls,
     )
     gained, handed = pairs(codes, ext, walls)
-    total = hand_back(gained, handed, over, chans, walls)
-    return total.reshape(1, 1, -1) * scale
+    held = hand_back(gained, handed, chans, walls)
+    return add_up(gained, held, over, scale, walls).reshape(1, 1, -1)
 
 
 def solution(mesh):

time: 40.5 us -> 38 us (0.938); the launches traced: 40.8 us -> 37.6 us
  Pallas kernels: 39.5 us -> 37.6 us
  other arithmetic: 1.33 us -> 0 us
    pallas_call x1, Pallas kernels: 9.93 us -> 8.09 us  [hand_back(): pl.pallas_call(functools.partial(return_kernel, chans, walls), out_shape=...]
    pallas_call x1, Pallas kernels: 17.9 us -> 16.3 us  [pairs(): pl.pallas_call(functools.partial(pair_kernel, walls), out_shape=(jax.Shap...]
    pallas_call x0 -> x1, Pallas kernels: none -> 1.51 us  [add_up(): pl.pallas_call(functools.partial(total_kernel, walls, scale), grid=(1,),...]
    mul x1 -> x0, other arithmetic: 1.33 us -> none  [on_device(): return total.reshape(1, 1, -1) * scale]
where the time goes in v1:
time: 38 us; the launch traced here: 37.6 us
  Pallas kernels  37.6 us (99%)
    pallas_call x1, Pallas kernels, pairs(): pl.pallas_call(functools.partial(pair_kernel, walls), out_shape=(jax.Shap...  16.3 us
    pallas_call x1, Pallas kernels, gather(): pl.pallas_call(functools.partial(gather_kernel, chans, walls), out_shape=...  11.7 us
    pallas_call x1, Pallas kernels, hand_back(): pl.pallas_call(functools.partial(return_kernel, chans, walls), out_shape=...  8.09 us
    pallas_call x1, Pallas kernels, add_up(): pl.pallas_call(functools.partial(total_kernel, walls, scale), grid=(1,),...  1.51 us

profile of v1, /device:TPU:0, one launch (start us, length us, event | category | flops | bytes accessed | tf_op | source)
XLA Modules:
  0.0 37.6 jit_solution(14892996278134693197)
XLA Ops:
  0.0 11.7 %shard_map.46 = (f32[7,2,64,128]{3,2,1,0:T(8,128)}, f32[2,16,256]{2,1,0:T(8,128)}, s32[16,128]{1,0:T(8,128)}) custom-call(f32[96,128]{1,0:T(8,128)} %bitcast.7, f32[32,128]{1,0:T(8,128)} %bitcast.8, s32[1,16]{1,0:T(1,128)} %bitcast.10, s32[5,2,16]{2,1,0:T(2,128)} %bitcast.9), custom_call_target="tpu_custom_call" | custom-call | tf_op jit(solution)/shard_map/pallas_call | solution.py:324
  11.7 16.3 %shard_map.47 = (f32[3,16,256]{2,1,0:T(8,128)}, f32[4,16,256]{2,1,0:T(8,128)}) custom-call(s32[16,128]{1,0:T(8,128)} %get-tuple-element.10.codes_in, f32[7,2,64,128]{3,2,1,0:T(8,128)} %get-tuple-element.11.far_ref), custom_call_target="tpu_custom_call" | custom-call | tf_op jit(solution)/shard_map/pallas_call | solution.py:665
  28.0 8.1 %shard_map.48.held_ref = f32[6,16,256]{2,1,0:T(8,128)} custom-call(f32[3,16,256]{2,1,0:T(8,128)} %get-tuple-element.12.gained_in.gained_ref, f32[4,16,256]{2,1,0:T(8,128)} %get-tuple-element.13.handed_in), custom_call_target="tpu_custom_call" | custom-call | tf_op jit(solution)/shard_map/pallas_call | solution.py:757
  36.1 1.5 %shard_map.49 = f32[32,128]{1,0:T(8,128)} custom-call(f32[3,16,256]{2,1,0:T(8,128)} %get-tuple-element.12.gained_in.gained_ref, f32[6,16,256]{2,1,0:T(8,128)} %shard_map.48.held_ref, f32[2,16,256]{2,1,0:T(8,128)} %get-tuple-element.14.over_ref), custom_call_target="tpu_custom_call" | custom-call | tf_op jit(solution)/shard_map/pallas_call | solution.py:792
